TPU v7x, 32 devices: a whole 2x2x4 slice. The times are simulated.
32 devices in a mesh: frag: 2 (over y), band: 8 (over z, x), slab: 2 (over core).
Axes of the slice: x: 2, y: 2, z: 4, core: 2. Of those that a mesh axis runs over, the one named last changes fastest.
Arguments:
- wavefunctions: bfloat16 [2048, 16384], P('band', ('frag', 'slab')), parts along dimension 1, may hold values from -6 to 6
- eigvec: bfloat16 [2048, 4096], P(None, ('frag', 'band', 'slab')), parts along dimension 1, may hold values from -1 to 1, as said below
- occupation: float32 [4096], P('frag'), parts along dimension 0, may hold values from 0.1 to 2
Outputs:
- rotated: float32 [2048, 16384], P('band', ('frag', 'slab')), parts along dimension 1
- density: float32 [16384], P(('frag', 'slab')), parts along dimension 0
There are 2 independent parts, one for each index of `frag`. A program takes and returns all parts, laid end to end along the dimension named above; each array names one. Nothing has to cross between parts.
Inputs may be any that keep to these rules, and one draw needn't show every extreme that they name: eigvec is an orthogonal matrix rounded to bfloat16.
All inputs are finite; a program needn't handle non-finite values.
Results may differ from a plain program's by a relative error of at most 0.0003.
Values may be sent and summed in bfloat16 or wider, within the bound.
A program may use at most 64 MiB of HBM per device.

v0:
```python
import jax
import jax.numpy as jnp
from jax import lax
from jax.sharding import PartitionSpec as P


def local(wavefunctions, eigvec, occupation):
    total_bands = eigvec.shape[0]
    by_points = lax.all_to_all(wavefunctions, "band", split_axis=1, concat_axis=0, tiled=True)
    point_rows = lax.dot_general(
        lax.all_gather(eigvec, ("band", "slab"), axis=1, tiled=True),
        by_points,
        (((0,), (0,)), ((), ())),
        preferred_element_type=jnp.float32,
    )
    rotated = lax.all_to_all(point_rows, "band", split_axis=0, concat_axis=1, tiled=True)
    local_density = jnp.dot(
        occupation,
        point_rows * point_rows,
        precision=lax.Precision.HIGHEST,
        preferred_element_type=jnp.float32,
    ) / jnp.float32(total_bands)
    density = lax.all_gather(local_density, "band", axis=0, tiled=True)
    return (rotated, density)


def solution(mesh):
    placed = (P("band", ("frag", "slab")), P(None, ("frag", "band", "slab")), P("frag"))
    return jax.shard_map(
        local,
        mesh=mesh,
        in_specs=placed,
        out_specs=(P("band", ("frag", "slab")), P(("frag", "slab"))),
        check_vma=False,
    )
```

profile of v0, /device:TPU:0, one launch (start us, length us, event | category | flops | bytes accessed | tf_op | source)
XLA Modules:
  0.0 261.2 jit_solution(3990064491963914201)
XLA Ops:
  7.2 0.0 copy-start
  7.2 0.0 all-gather.3.cloned.1.call-start
  7.2 0.7 all-gather.3.cloned.1.call-update
  7.9 4.1 %copy.10 = bf16[256,4096]{0,1:T(8,128)(2,1)} copy(bf16[256,4096]{1,0:T(8,128)(2,1)} %param.3) | data formatting | bytes 4194304 | tf_op args[0]
  12.0 93.2 %all_to_all.38 = bf16[256,8,512]{0,2,1:T(8,128)(2,1)S(1)} all-to-all(bf16[256,8,512]{0,2,1:T(8,128)(2,1)} %bitcast.17), channel_id=1, replica_groups=mesh['frag'=2,'band'=8,'slab'=2] {'band'}, dimensions={1} | all-to-all | bytes 4194304 | tf_op jit(solution)/shard_map/all_to_all | solution.py:9
  105.2 2.4 copy.11
  107.6 13.8 %all-gather.3.cloned.1.call-done = bf16[2048,2048]{1,0:T(8,128)(2,1)} async-done(((bf16[2048,128]{1,0:T(8,128)(2,1)}), bf16[2048,2048]{1,0:T(8,128)(2,1)}) %all-gather.3.cloned.1.call-update) | async-done | bytes 8388624 | tf_op jit(solution)/shard_map/all_gather | solution.py:11
  121.4 10.5 %fusion.2 = f32[2048,512]{1,0:T(8,128)} fusion(bf16[2048,2048]{1,0:T(8,128)(2,1)} %all-gather.3.cloned.1.call-done, bf16[2048,512]{1,0:T(8,128)(2,1)} %bitcast.19), kind=kOutput, calls=%fused_computation.3 | convolution fusion | flops 4294967296 | bytes 14680064 | tf_op jit(solution)/shard_map/dot_general | solution.py:10
  132.0 4.5 %all-to-all-start.1 = ((f32[8,256,512]{2,1,0:T(8,128)}), f32[8,256,512]{2,1,0:T(8,128)}, u32[]{:S(2)}, u32[]{:S(2)}) async-start(f32[8,256,512]{2,1,0:T(8,128)} %bitcast.15), calls=%async_computation.1 | async-start | bytes 8388608 | tf_op jit(solution)/shard_map/all_to_all | solution.py:16
  136.5 0.0 copy-done
  136.6 4.6 %fusion = f32[1,512]{1,0:T(1,128)S(1)} fusion(f32[2048,1]{0,1:T(1,128)S(1)} %bitcast.14, f32[2048,512]{1,0:T(8,128)} %fusion.2), kind=kOutput, calls=%fused_computation | convolution fusion | flops 13631488 | bytes 4204544 | tf_op jit(solution)/shard_map/dot_general | solution.py:17
  141.1 107.8 %all-gather = f32[8,1,512]{2,1,0:T(1,128)S(1)} all-gather(f32[1,1,512]{2,1,0:T(1,128)S(1)} %bitcast.22), channel_id=1, replica_groups=mesh['frag'=2,'band'=8,'slab'=2] {'band'}, dimensions={0}, use_global_device_ids=true | all-gather | bytes 18432 | tf_op jit(solution)/shard_map/all_gather | solution.py:23
  248.9 0.0 all-to-all-done.1
  248.9 4.8 %copy.13 = f32[8,32,8,512]{3,2,0,1:T(8,128)} copy(f32[8,32,8,512]{3,2,1,0:T(8,128)} %bitcast.9) | data formatting | bytes 8388608 | tf_op jit(solution)/shard_map/all_to_all | solution.py:16
  253.8 0.6 copy.15
  (1 shorter events, 0.0 us)
Async XLA Ops:
  7.2 129.4 %copy-start = (f32[2048]{0:T(1024)S(1)}, f32[2048]{0:T(1024)}, u32[]{:S(2)}) copy-start(f32[2048]{0:T(1024)} %param.5) | copy-start | bytes 24580
  7.2 114.3 %all-gather.3.cloned.1.call-start = ((), (), s32[]{:S(2)}) async-start(), calls=%async_computation.2 | async-start | bytes 8912896 | tf_op jit(solution)/shard_map/all_gather | solution.py:11
  132.0 116.9 %all-to-all-start.1 = ((f32[8,256,512]{2,1,0:T(8,128)}), f32[8,256,512]{2,1,0:T(8,128)}, u32[]{:S(2)}, u32[]{:S(2)}) async-start(f32[8,256,512]{2,1,0:T(8,128)} %bitcast.15), calls=%async_computation.1 | async-start | bytes 8388608 | tf_op jit(solution)/shard_map/all_to_all | solution.py:16
Sparse Core Ops, SparseCore 0:
  10.1 111.2 all-gather.2
where the time goes:
time: 262 us; the launch traced here: 261 us
  blocking collectives  201 us (77%)
  matrix products  15.1 us (6%)
  waiting for transfers between devices  14.5 us (6%)
  between operations  14.1 us (5%)
  local copies, waits for them, and re-layouts  11.9 us (5%)
  starting transfers between devices  4.58 us (2%)
    all_gather x1, blocking collectives, local(): density = lax.all_gather(local_density, 'band', axis=0, tiled=True)  108 us
    all_to_all x1, blocking collectives, local(): lax.all_to_all(wavefunctions, 'band', split_axis=1, concat_axis=0, tiled=...  93.2 us
    all_gather x1, waiting for transfers between devices, local(): lax.all_gather(eigvec, ('band', 'slab'), axis=1, tiled=True)  13.8 us
    dot_general x1, matrix products, local(): lax.dot_general(lax.all_gather(eigvec, ('band', 'slab'), axis=1, tiled=Tr...  10.5 us
  transfers between devices with their start and end apart: 2, of which 1 were waited for; matrix products, arithmetic and copies ran while one was open for 4% of the time, Pallas kernels for 0%

commit v1 on v0

--- a/solution.py
+++ b/solution.py
@@ -1,10 +1,18 @@
+import functools
+
 import jax
 import jax.numpy as jnp
 from jax import lax
+from jax.experimental import pallas as pl
+from jax.experimental.pallas import tpu as pltpu
 from jax.sharding import PartitionSpec as P
 
-
-def local(wavefunctions, eigvec, occupation):
+MESH = pl.DeviceIdType.MESH
+LANES = 128
+AHEAD = 5
+
+
+def plain(wavefunctions, eigvec, occupation):
     total_bands = eigvec.shape[0]
     by_points = lax.all_to_all(wavefunctions, "band", split_axis=1, concat_axis=0, tiled=True)
     point_rows = lax.dot_general(
@@ -24,10 +32,235 @@
     return (rotated, density)
 
 
+def kernel(nb, wave, panel, weight, out, density, gathered, vectors, staged, part, parts, zrecv, up, down, xrecv, xsend, own, erecv, esend, orecv, osend, drecv, dsend):
+    nz = nb // 2
+    frag, band, slab = (lax.axis_index(name) for name in ("frag", "band", "slab"))
+    z, x = band // 2, lax.rem(band, 2)
+    rows, points = wave.shape
+    half = points // 2
+    steps = half // LANES
+    width = panel.shape[0]
+    total_bands = panel.shape[1]
+
+    def at(b, s=slab):
+        return (frag, b, s)
+
+    beside = 2 * z + 1 - x
+    above, below = lax.rem(band + 2, nb), lax.rem(band + nb - 2, nb)
+
+    barrier = pltpu.get_barrier_semaphore()
+    for hop in range(1, nb):
+        pl.semaphore_signal(barrier, inc=1, device_id=at(lax.rem(band + hop, nb)), device_id_type=MESH)
+    for target in (at(band, 1 - slab), at(beside, 1 - slab)):
+        pl.semaphore_signal(barrier, inc=1, device_id=target, device_id_type=MESH)
+    pl.semaphore_wait(barrier, nb + 1)
+
+    def send(src, dst, ssem, rsem, target):
+        return pltpu.make_async_remote_copy(
+            src_ref=src, dst_ref=dst, send_sem=ssem, recv_sem=rsem, device_id=target, device_id_type=MESH
+        )
+
+    def columns(of, step):
+        return pl.ds(pl.multiple_of(of * half + step * LANES, LANES), LANES)
+
+    mine = vectors.at[pl.ds(pl.multiple_of((2 * x + slab) * width, width), width)]
+
+    def vector_copy(i, target):
+        return send(panel, mine, esend.at[i], erecv.at[2 * x + slab], target)
+
+    def vector_from(x2, s2):
+        there = vectors.at[pl.ds(pl.multiple_of((2 * x2 + s2) * width, width), width)]
+        return send(there, there, esend.at[0], erecv.at[2 * x2 + s2], at(band, 1 - slab))
+
+    def across(step):
+        return send(wave.at[:, columns(1 - x, step)], gathered.at[step, band], xsend.at[step], xrecv.at[step], at(beside))
+
+    def across_from(step):
+        there = gathered.at[step, beside]
+        return send(there, there, xsend.at[step], xrecv.at[step], at(beside))
+
+    def keep(step):
+        return pltpu.make_async_copy(wave.at[:, columns(x, step)], gathered.at[step, band], own.at[step])
+
+    def pair(step, origin, sems, target):
+        both = gathered.at[step, pl.ds(2 * origin, 2)]
+        return send(both, both, sems.at[step, origin], zrecv.at[step, origin], at(target))
+
+    def result(step):
+        return send(staged.at[step], out.at[:, columns(x, step)], osend.at[step], orecv.at[step], at(beside))
+
+    def result_from(step):
+        there = out.at[:, columns(1 - x, step)]
+        return send(there, there, osend.at[step], orecv.at[step], at(beside))
+
+    copies = [
+        vector_copy(0, at(band, 1 - slab)),
+        vector_copy(1, at(beside)),
+        vector_copy(2, at(beside, 1 - slab)),
+    ]
+
+    def begin(step, _):
+        across(step).start()
+        keep(step).start()
+        return _
+
+    lax.fori_loop(0, AHEAD, begin, 0)
+    for copy in copies:
+        copy.start()
+    home = pltpu.make_async_copy(panel, mine, own.at[steps])
+    home.start()
+    lax.fori_loop(AHEAD, steps, begin, 0)
+
+    def spread(step):
+        keep(step).wait()
+        across_from(step).wait_recv()
+
+        @pl.when(z < nz - 1)
+        def _():
+            pair(step, z, up, above).start()
+
+        @pl.when(z > 0)
+        def _():
+            pair(step, z, down, below).start()
+
+    def collect(step):
+        for distance in range(1, nz):
+            @pl.when(z + distance < nz)
+            def _():
+                pair(step, z + distance, down, above).wait_recv()
+
+                @pl.when(z > 0)
+                def _():
+                    pair(step, z + distance, down, below).start()
+
+            @pl.when(z - distance >= 0)
+            def _():
+                pair(step, z - distance, up, below).wait_recv()
+
+                @pl.when(z < nz - 1)
+                def _():
+                    pair(step, z - distance, up, above).start()
+
+    def compute(step):
+        block = gathered[step].reshape(nb * rows, LANES)
+        here, there = rows * x, rows * (1 - x)
+        kept = jnp.dot(vectors[pl.ds(pl.multiple_of(here, rows), rows), :], block, preferred_element_type=jnp.float32)
+        sent = jnp.dot(vectors[pl.ds(pl.multiple_of(there, rows), rows), :], block, preferred_element_type=jnp.float32)
+        staged[step] = sent
+        out[:, columns(x, step)] = kept
+        sums = jnp.sum(weight[pl.ds(pl.multiple_of(here, rows), rows), :] * kept * kept, axis=0, keepdims=True)
+        sums = sums + jnp.sum(weight[pl.ds(pl.multiple_of(there, rows), rows), :] * sent * sent, axis=0, keepdims=True)
+        part[0, :, pl.ds(pl.multiple_of(step * LANES, LANES), LANES)] = sums
+        result(step).start()
+
+    def first(step, carry):
+        spread(step)
+        return carry
+
+    lax.fori_loop(0, AHEAD, first, 0)
+    home.wait()
+    for hop in range(1, 4):
+        x2 = x if hop == 1 else 1 - x
+        s2 = slab if hop == 2 else 1 - slab
+        vector_from(x2, s2).wait_recv()
+
+    def body(step, carry):
+        @pl.when(step + AHEAD < steps)
+        def _():
+            spread(step + AHEAD)
+
+        collect(step)
+        compute(step)
+        return carry
+
+    lax.fori_loop(0, steps, body, 0)
+
+    def share(hop):
+        target = lax.rem(band + hop, nb)
+        return send(part.at[0], parts.at[band], dsend.at[hop], drecv.at[band], at(target))
+
+    for hop in range(1, nb):
+        share(hop).start()
+    parts[band] = part[0]
+
+    def finish(step, carry):
+        result_from(step).wait_recv()
+        result(step).wait_send()
+        across(step).wait_send()
+        for origin in range(nz):
+            @pl.when((z < nz - 1) & (origin <= z))
+            def _():
+                pair(step, origin, up, above).wait_send()
+
+            @pl.when((z > 0) & (origin >= z))
+            def _():
+                pair(step, origin, down, below).wait_send()
+
+        return carry
+
+    lax.fori_loop(0, steps, finish, 0)
+    for copy in copies:
+        copy.wait_send()
+    for hop in range(1, nb):
+        share(hop).wait_send()
+        source = lax.rem(band + nb - hop, nb)
+        send(parts.at[source], parts.at[source], dsend.at[hop], drecv.at[source], at(source)).wait_recv()
+    for side in range(2):
+        total = parts[side]
+        for level in range(1, nz):
+            total = total + parts[2 * level + side]
+        density[side] = total / jnp.float32(total_bands)
+
+
+def local(nb, wavefunctions, eigvec, occupation):
+    rows, points = wavefunctions.shape
+    total_bands, width = eigvec.shape
+    if nb % 2 or width % LANES or rows != 2 * width or points % (2 * LANES) or points // 2 // LANES <= AHEAD:
+        return plain(wavefunctions, eigvec, occupation)
+    nz, half = nb // 2, points // 2
+    steps = half // LANES
+    weights = lax.dynamic_slice(occupation, (lax.axis_index("band") // 2 * (2 * rows),), (2 * rows,))
+    weights = jnp.broadcast_to(weights[:, None], (2 * rows, LANES))
+    vmem = pl.BlockSpec(memory_space=pltpu.VMEM)
+    dma = pltpu.SemaphoreType.DMA
+    rotated, density = pl.pallas_call(
+        functools.partial(kernel, nb),
+        out_shape=(
+            jax.ShapeDtypeStruct((rows, points), jnp.float32),
+            jax.ShapeDtypeStruct((2, 1, half), jnp.float32),
+        ),
+        in_specs=[vmem] * 3,
+        out_specs=(vmem, vmem),
+        scratch_shapes=[
+            pltpu.VMEM((steps, nb, rows, LANES), jnp.bfloat16),
+            pltpu.VMEM((2 * rows, total_bands), jnp.bfloat16),
+            pltpu.VMEM((steps, rows, LANES), jnp.float32),
+            pltpu.VMEM((1, 1, half), jnp.float32),
+            pltpu.VMEM((nb, 1, half), jnp.float32),
+            dma((steps, nz)),
+            dma((steps, nz)),
+            dma((steps, nz)),
+            dma((steps,)),
+            dma((steps,)),
+            dma((steps + 1,)),
+            dma((4,)),
+            dma((3,)),
+            dma((steps,)),
+            dma((steps,)),
+            dma((nb,)),
+            dma((nb,)),
+        ],
+        compiler_params=pltpu.CompilerParams(
+            collective_id=0, has_side_effects=True, vmem_limit_bytes=56 * 2**20
+        ),
+    )(wavefunctions, eigvec.T, weights)
+    return (rotated, density.reshape(points))
+
+
 def solution(mesh):
     placed = (P("band", ("frag", "slab")), P(None, ("frag", "band", "slab")), P("frag"))
     return jax.shard_map(
-        local,
+        functools.partial(local, mesh.shape["band"]),
         mesh=mesh,
         in_specs=placed,
         out_specs=(P("band", ("frag", "slab")), P(("frag", "slab"))),

time: 262 us -> 182 us (0.69)
  blocking collectives: 201 us -> 0 us
  Pallas kernels: 0 us -> 172 us
  matrix products: 15.1 us -> 0 us
  waiting for transfers between devices: 14.5 us -> 0 us
  between operations: 14.1 us -> 0.67 us
  starting transfers between devices: 4.58 us -> 0 us
  local copies, waits for them, and re-layouts: 11.9 us -> 8.91 us
    pallas_call x0 -> x1, Pallas kernels: none -> 172 us  [local(): pl.pallas_call(functools.partial(kernel, nb), out_shape=(jax.ShapeDtypeSt...]
    all_gather x1 -> x0, blocking collectives: 108 us -> none  [local(): density = lax.all_gather(local_density, 'band', axis=0, tiled=True)]
    all_to_all x1 -> x0, blocking collectives: 93.2 us -> none  [local(): lax.all_to_all(wavefunctions, 'band', split_axis=1, concat_axis=0, tiled=...]
    dot_general x2 -> x0, matrix products: 15.1 us -> none  [the longest x1 10.5 us: local(): lax.dot_general(lax.all_gather(eigvec, ('band', 'slab'), axis=1, tiled=Tr...]
    all_gather x1 -> x0, waiting for transfers between devices: 13.8 us -> none  [local(): lax.all_gather(eigvec, ('band', 'slab'), axis=1, tiled=True)]
    all_to_all x2 -> x0, local copies, waits for them, and re-layouts: 7.25 us -> none  [the longest x1 4.84 us: local(): lax.all_to_all(point_rows, 'band', split_axis=0, concat_axis=1, tiled=True)]
    all_to_all x1 -> x0, starting transfers between devices: 4.54 us -> none  [local(): lax.all_to_all(point_rows, 'band', split_axis=0, concat_axis=1, tiled=True)]
    unnamed x4 -> x5, local copies, waits for them, and re-layouts: 4.69 us -> 7.31 us
  transfers between devices with their start and end apart: 2 -> 0, of which waited for: 1 -> 0; matrix products, arithmetic and copies ran while one was open for 4% -> 0% of each run, Pallas kernels for 0% -> 0%
where the time goes in v1:
time: 182 us; the launch traced here: 181 us
  Pallas kernels  172 us (95%)
  local copies, waits for them, and re-layouts  8.91 us (5%)
    pallas_call x1, Pallas kernels, local(): pl.pallas_call(functools.partial(kernel, nb), out_shape=(jax.ShapeDtypeSt...  172 us
    unnamed x5, local copies, waits for them, and re-layouts  7.31 us

profile of v1, /device:TPU:0, one launch (start us, length us, event | category | flops | bytes accessed | tf_op | source)
XLA Modules:
  0.0 181.4 jit_solution(6603292524788149468)
XLA Ops:
  0.6 0.8 dynamic_slice.3
  1.4 0.8 broadcast_in_dim.2.weight
  2.2 2.0 %copy.5 = bf16[2048,128]{0,1:T(8,128)(2,1)} copy(bf16[2048,128]{1,0:T(8,128)(2,1)} %param.4) | data formatting | bytes 1048576 | tf_op args[1]
  4.3 171.8 %shard_map.50 = (f32[256,4096]{1,0:T(8,128)}, f32[2,1,2048]{2,1,0:T(1,128)}) custom-call(bf16[256,4096]{1,0:T(8,128)(2,1)} %wave.1, bf16[128,2048]{1,0:T(8,128)(2,1)} %bitcast.2, f32[512,128]{1,0:T(8,128)} %broadcast_in_dim.2.weight), custom_call_target="tpu_custom_call" | custom-call | tf_op jit(solution)/shard_map/pallas_call | solution.py:226
  176.1 0.0 copy-start
  176.1 4.7 %copy.8 = f32[256,4096]{1,0:T(8,128)} copy(f32[256,4096]{1,0:T(8,128)} %get-tuple-element.8) | data formatting | bytes 8388608
  180.7 0.0 copy-done
  180.7 0.6 copy.9
Async XLA Ops:
  176.1 4.7 %copy-start = (f32[2,1,2048]{2,1,0:T(1,128)S(1)}, f32[2,1,2048]{2,1,0:T(1,128)}, u32[]{:S(2)}) copy-start(f32[2,1,2048]{2,1,0:T(1,128)} %get-tuple-element.5) | copy-start | bytes 49156

commit v2 on v1

--- a/solution.py
+++ b/solution.py
@@ -9,7 +9,7 @@
 
 MESH = pl.DeviceIdType.MESH
 LANES = 128
-AHEAD = 5
+AHEAD = 10
 
 
 def plain(wavefunctions, eigvec, occupation):
@@ -96,8 +96,9 @@
     copies = [
         vector_copy(0, at(band, 1 - slab)),
         vector_copy(1, at(beside)),
-        vector_copy(2, at(beside, 1 - slab)),
     ]
+    passed = vectors.at[pl.ds(pl.multiple_of((2 * (1 - x) + slab) * width, width), width)]
+    relay = send(passed, passed, esend.at[2], erecv.at[2 * (1 - x) + slab], at(band, 1 - slab))
 
     def begin(step, _):
         across(step).start()
@@ -159,10 +160,10 @@
 
     lax.fori_loop(0, AHEAD, first, 0)
     home.wait()
-    for hop in range(1, 4):
-        x2 = x if hop == 1 else 1 - x
-        s2 = slab if hop == 2 else 1 - slab
-        vector_from(x2, s2).wait_recv()
+    vector_from(1 - x, slab).wait_recv()
+    relay.start()
+    vector_from(x, 1 - slab).wait_recv()
+    vector_from(1 - x, 1 - slab).wait_recv()
 
     def body(step, carry):
         @pl.when(step + AHEAD < steps)
@@ -199,7 +200,7 @@
         return carry
 
     lax.fori_loop(0, steps, finish, 0)
-    for copy in copies:
+    for copy in (*copies, relay):
         copy.wait_send()
     for hop in range(1, nb):
         share(hop).wait_send()

time: 182 us -> 167 us (0.918)
  Pallas kernels: 172 us -> 157 us
    pallas_call x1, Pallas kernels: 172 us -> 157 us  [local(): pl.pallas_call(functools.partial(kernel, nb), out_shape=(jax.ShapeDtypeSt...]
where the time goes in v2:
time: 167 us
  Pallas kernels  157 us (94%)
  local copies, waits for them, and re-layouts  8.91 us (5%)
    pallas_call x1, Pallas kernels, local(): pl.pallas_call(functools.partial(kernel, nb), out_shape=(jax.ShapeDtypeSt...  157 us
    unnamed x5, local copies, waits for them, and re-layouts  7.31 us

profile of v2, /device:TPU:0, one launch (start us, length us, event | category | flops | bytes accessed | tf_op | source)
XLA Modules:
  0.0 167.0 jit_solution(14705750684276504776)
XLA Ops:
  0.6 0.8 dynamic_slice.3
  1.4 0.8 broadcast_in_dim.2.weight
  2.2 2.0 %copy.5 = bf16[2048,128]{0,1:T(8,128)(2,1)} copy(bf16[2048,128]{1,0:T(8,128)(2,1)} %param.4) | data formatting | bytes 1048576 | tf_op args[1]
  4.3 157.5 %shard_map.50 = (f32[256,4096]{1,0:T(8,128)}, f32[2,1,2048]{2,1,0:T(1,128)}) custom-call(bf16[256,4096]{1,0:T(8,128)(2,1)} %wave.1, bf16[128,2048]{1,0:T(8,128)(2,1)} %bitcast.2, f32[512,128]{1,0:T(8,128)} %broadcast_in_dim.2.weight), custom_call_target="tpu_custom_call" | custom-call | tf_op jit(solution)/shard_map/pallas_call | solution.py:227
  161.8 0.0 copy-start
  161.8 4.7 %copy.8 = f32[256,4096]{1,0:T(8,128)} copy(f32[256,4096]{1,0:T(8,128)} %get-tuple-element.8) | data formatting | bytes 8388608
  166.4 0.0 copy-done
  166.4 0.6 copy.9
Async XLA Ops:
  161.8 4.7 %copy-start = (f32[2,1,2048]{2,1,0:T(1,128)S(1)}, f32[2,1,2048]{2,1,0:T(1,128)}, u32[]{:S(2)}) copy-start(f32[2,1,2048]{2,1,0:T(1,128)} %get-tuple-element.5) | copy-start | bytes 49156
